TPU v7x, 256 devices: a 4x2x16 block of a 4x16x16 slice. The times are simulated.
256 devices in a mesh: grp: 2 (over y), mode: 64 (over x, z), node: 2 (over core).
Axes of the slice: x: 4, y: 2, z: 16, core: 2. Of those that a mesh axis runs over, the one named last changes fastest.
The devices are a block of a 4x16x16 slice.
Arguments:
- mode_basis: float32 [4096, 32768], P('mode', 'node'), may hold values from -16 to 16
- mode_scales: float32 [4096], P('mode'), may hold values from 0.003 to 0.02
- mean_log: float32 [32768], P(('node', 'mode')), may hold values from -0.5 to 0.5
- sample_seeds: int32 [4096], P('grp'), parts along dimension 0, may hold values from 0 to 1073741823
Outputs:
- modulus: float32 [32768, 4096], P(('node', 'mode'), 'grp'), parts along dimension 1
- sample_means: float32 [4096], P('grp'), parts along dimension 0
There are 2 independent parts, one for each index of `grp`. A program takes and returns all parts, laid end to end along the dimension named above; an argument that names none is the same for every part. Nothing has to cross between parts.
All inputs are finite; a program needn't handle non-finite values.
Results may differ from a plain program's by a relative error of at most 0.00005.
Values sent between devices are 32-bit elements; how exact they have to be, the bound alone decides.
A program may use at most 64 MiB of HBM per device.

v0:
```python
import functools
import math

import jax
import jax.numpy as jnp
from jax import lax
from jax.sharding import Mesh
from jax.sharding import PartitionSpec as P

MODE = ("mode_0", "mode_1")
MODE_NODE = ("mode_0", "mode_1", "node")
NODE_MODE = ("node", "mode_0", "mode_1")


def over_axes(array, axes):
    return functools.reduce(lax.psum, axes, array)


def scramble(seed_words, counter_words):
    mixed_word = seed_words * -1640531527 + counter_words * 668265261
    mixed_word = mixed_word ^ mixed_word >> 15 & 131071
    mixed_word = mixed_word * -2048144789
    mixed_word = mixed_word ^ mixed_word >> 13 & 524287
    mixed_word = mixed_word * -1028477387
    mixed_word = mixed_word ^ mixed_word >> 16 & 65535
    return mixed_word


def normals(sample_seeds, mode_start, mode_count):
    mode_ids = mode_start + jnp.arange(mode_count, dtype=jnp.int32)
    seed_words = sample_seeds[None, :]
    counter_words = (2 * mode_ids)[:, None]
    first_word = scramble(seed_words, counter_words)
    second_word = scramble(seed_words, counter_words + 1)
    first_unit = ((first_word & 16777215).astype(jnp.float32) + 0.5) * (1.0 / 16777216.0)
    second_unit = ((second_word & 16777215).astype(jnp.float32) + 0.5) * (1.0 / 16777216.0)
    radius = jnp.sqrt(-2.0 * jnp.log(first_unit))
    return radius * jnp.cos(2.0 * math.pi * second_unit)


def contract_all(all_modes, sample_seeds):
    mode_total = all_modes.shape[0]
    block_modes = min(512, mode_total)
    block_count = mode_total // block_modes
    start_total = jnp.zeros((all_modes.shape[1], sample_seeds.shape[0]), jnp.float32)

    def add_block(block, total):
        first_mode = (block * block_modes).astype(jnp.int32)
        rows = lax.dynamic_slice_in_dim(all_modes, first_mode, block_modes, 0)
        coeffs = normals(sample_seeds, first_mode, block_modes)
        return total + lax.dot_general(
            rows,
            coeffs,
            (((0,), (0,)), ((), ())),
            precision=lax.Precision.HIGHEST,
            preferred_element_type=jnp.float32,
        )

    return lax.fori_loop(0, block_count, add_block, start_total)


def on_device(mode_basis, mode_scales, mean_log, sample_seeds):
    own_rows = mean_log.shape[0]
    scaled = mode_scales[:, None] * mode_basis
    gathered = lax.all_to_all(scaled, MODE, split_axis=1, concat_axis=0, tiled=True)
    summed = contract_all(gathered, sample_seeds)
    modulus = jnp.exp(mean_log[:, None] + summed)
    totals = over_axes(jnp.sum(modulus, axis=0), MODE_NODE)
    node_count = own_rows * lax.axis_size(MODE) * lax.axis_size("node")
    return (modulus, totals / node_count)


def solution(mesh):
    finer = Mesh(
        mesh.devices.reshape(mesh.shape["grp"], 4, 16, mesh.shape["node"]),
        ("grp", "mode_0", "mode_1", "node"),
    )
    in_specs = (P(MODE, "node"), P(MODE), P(NODE_MODE), P("grp"))
    out_specs = (P(NODE_MODE, "grp"), P("grp"))
    return jax.shard_map(
        on_device, mesh=finer, in_specs=in_specs, out_specs=out_specs, check_vma=False
    )
```

profile of v0, /device:TPU:33, one launch (start us, length us, event | category | flops | bytes accessed | tf_op | source)
XLA Modules:
  0.0 460.9 jit_solution(5914141611776023181)
XLA Ops:
  0.6 2.5 broadcast_multiply_fusion.1
  3.2 2.6 copy.9
  5.8 0.0 copy-start
  5.8 29.7 %all-to-all-start = ((f32[64,64,256]{2,0,1:T(8,128)}), f32[64,64,256]{2,0,1:T(8,128)}, u32[]{:S(2)}, u32[]{:S(2)}) async-start(f32[64,64,256]{2,0,1:T(8,128)} %bitcast.7), calls=%async_computation | async-start | bytes 8388608 | tf_op jit(solution)/shard_map/all_to_all | solution.py:65
  35.5 182.5 %all-to-all-done = f32[64,64,256]{2,0,1:T(8,128)} async-done(((f32[64,64,256]{2,0,1:T(8,128)}), f32[64,64,256]{2,0,1:T(8,128)}, u32[]{:S(2)}, u32[]{:S(2)}) %all-to-all-start) | async-done | bytes 4194336 | tf_op jit(solution)/shard_map/all_to_all | solution.py:65
  218.0 0.0 copy-done
  218.0 0.0 copy-start.1
  218.0 194.2 %while.16 = (s32[]{:T(128)}, f32[256,2048]{1,0:T(8,128)S(1)}, f32[4096,256]{1,0:T(8,128)}, s32[2048]{0:T(1024)S(1)}, s32[]{:T(128)}, /*index=5*/s32[]{:T(128)}, s32[]{:T(128)}, s32[]{:T(128)}) while((s32[]{:T(128)}, f32[256,2048]{1,0:T(8,128)S(1)}, f32[4096,256]{1,0:T(8,128)}, s32[2048]{0:T(1024)S(1)}, s32[]{:T(128)}, ...), condition=%wide.region_1.0_spmd.clone, body=%wide.region_0.0_spmd.clone.sunk | while | flops 3257930240 | bytes 4751509 | solution.py:59
  218.0 24.2 %fusion.75 = f32[256,2048]{1,0:T(8,128)S(1)} fusion(f32[256,2048]{1,0:T(8,128)S(1)} %get-tuple-element.179, s32[512]{0:T(512)S(1)} %get-tuple-element.168, s32[512]{0:T(512)S(1)} %get-tuple-element.169, s32[2048]{0:T(1024)S(1)} %broadcast_multiply_fusion.4, pred[]{:T(512)S(6)} %compare.3, f32[4096,256]{1,0:T(8,128)} %get-tuple-element.188, ...), kind=kOutput, calls=%fused_computation.36.clone.1 | convolution fusion | flops 3257925632 | bytes 4730885 | tf_op jit(solution)/shard_map/while/body/eval_jaxpr/dot_general | solution.py:51
  242.3 24.2 %fusion.75 = f32[256,2048]{1,0:T(8,128)S(1)} fusion(f32[256,2048]{1,0:T(8,128)S(1)} %get-tuple-element.179, s32[512]{0:T(512)S(1)} %get-tuple-element.168, s32[512]{0:T(512)S(1)} %get-tuple-element.169, s32[2048]{0:T(1024)S(1)} %broadcast_multiply_fusion.4, pred[]{:T(512)S(6)} %compare.3, f32[4096,256]{1,0:T(8,128)} %get-tuple-element.188, ...), kind=kOutput, calls=%fused_computation.36.clone.1 | convolution fusion | flops 3257925632 | bytes 4730885 | tf_op jit(solution)/shard_map/while/body/eval_jaxpr/dot_general | solution.py:51
  266.6 24.2 %fusion.75 = f32[256,2048]{1,0:T(8,128)S(1)} fusion(f32[256,2048]{1,0:T(8,128)S(1)} %get-tuple-element.179, s32[512]{0:T(512)S(1)} %get-tuple-element.168, s32[512]{0:T(512)S(1)} %get-tuple-element.169, s32[2048]{0:T(1024)S(1)} %broadcast_multiply_fusion.4, pred[]{:T(512)S(6)} %compare.3, f32[4096,256]{1,0:T(8,128)} %get-tuple-element.188, ...), kind=kOutput, calls=%fused_computation.36.clone.1 | convolution fusion | flops 3257925632 | bytes 4730885 | tf_op jit(solution)/shard_map/while/body/eval_jaxpr/dot_general | solution.py:51
  290.9 24.2 %fusion.75 = f32[256,2048]{1,0:T(8,128)S(1)} fusion(f32[256,2048]{1,0:T(8,128)S(1)} %get-tuple-element.179, s32[512]{0:T(512)S(1)} %get-tuple-element.168, s32[512]{0:T(512)S(1)} %get-tuple-element.169, s32[2048]{0:T(1024)S(1)} %broadcast_multiply_fusion.4, pred[]{:T(512)S(6)} %compare.3, f32[4096,256]{1,0:T(8,128)} %get-tuple-element.188, ...), kind=kOutput, calls=%fused_computation.36.clone.1 | convolution fusion | flops 3257925632 | bytes 4730885 | tf_op jit(solution)/shard_map/while/body/eval_jaxpr/dot_general | solution.py:51
  315.1 24.2 %fusion.75 = f32[256,2048]{1,0:T(8,128)S(1)} fusion(f32[256,2048]{1,0:T(8,128)S(1)} %get-tuple-element.179, s32[512]{0:T(512)S(1)} %get-tuple-element.168, s32[512]{0:T(512)S(1)} %get-tuple-element.169, s32[2048]{0:T(1024)S(1)} %broadcast_multiply_fusion.4, pred[]{:T(512)S(6)} %compare.3, f32[4096,256]{1,0:T(8,128)} %get-tuple-element.188, ...), kind=kOutput, calls=%fused_computation.36.clone.1 | convolution fusion | flops 3257925632 | bytes 4730885 | tf_op jit(solution)/shard_map/while/body/eval_jaxpr/dot_general | solution.py:51
  339.4 24.2 %fusion.75 = f32[256,2048]{1,0:T(8,128)S(1)} fusion(f32[256,2048]{1,0:T(8,128)S(1)} %get-tuple-element.179, s32[512]{0:T(512)S(1)} %get-tuple-element.168, s32[512]{0:T(512)S(1)} %get-tuple-element.169, s32[2048]{0:T(1024)S(1)} %broadcast_multiply_fusion.4, pred[]{:T(512)S(6)} %compare.3, f32[4096,256]{1,0:T(8,128)} %get-tuple-element.188, ...), kind=kOutput, calls=%fused_computation.36.clone.1 | convolution fusion | flops 3257925632 | bytes 4730885 | tf_op jit(solution)/shard_map/while/body/eval_jaxpr/dot_general | solution.py:51
  363.7 24.2 %fusion.75 = f32[256,2048]{1,0:T(8,128)S(1)} fusion(f32[256,2048]{1,0:T(8,128)S(1)} %get-tuple-element.179, s32[512]{0:T(512)S(1)} %get-tuple-element.168, s32[512]{0:T(512)S(1)} %get-tuple-element.169, s32[2048]{0:T(1024)S(1)} %broadcast_multiply_fusion.4, pred[]{:T(512)S(6)} %compare.3, f32[4096,256]{1,0:T(8,128)} %get-tuple-element.188, ...), kind=kOutput, calls=%fused_computation.36.clone.1 | convolution fusion | flops 3257925632 | bytes 4730885 | tf_op jit(solution)/shard_map/while/body/eval_jaxpr/dot_general | solution.py:51
  388.0 24.2 %fusion.75 = f32[256,2048]{1,0:T(8,128)S(1)} fusion(f32[256,2048]{1,0:T(8,128)S(1)} %get-tuple-element.179, s32[512]{0:T(512)S(1)} %get-tuple-element.168, s32[512]{0:T(512)S(1)} %get-tuple-element.169, s32[2048]{0:T(1024)S(1)} %broadcast_multiply_fusion.4, pred[]{:T(512)S(6)} %compare.3, f32[4096,256]{1,0:T(8,128)} %get-tuple-element.188, ...), kind=kOutput, calls=%fused_computation.36.clone.1 | convolution fusion | flops 3257925632 | bytes 4730885 | tf_op jit(solution)/shard_map/while/body/eval_jaxpr/dot_general | solution.py:51
  412.2 0.0 copy-done.1
  412.2 1.7 fusion.69
  413.9 7.0 %psum.21 = f32[2048]{0:T(1024)S(1)} all-reduce(f32[2048]{0:T(1024)S(1)} %get-tuple-element.137), channel_id=1, replica_groups=mesh['grp'=2,'mode_0'=4,'mode_1'=16,'node'=2] {'mode_0'}, use_global_device_ids=true, to_apply=%region_3.0 | all-reduce | flops 2048 | bytes 16384 | tf_op jit(solution)/shard_map/psum | solution.py:16
  420.9 27.1 %psum.22 = f32[2048]{0:T(1024)S(1)} all-reduce(f32[2048]{0:T(1024)S(1)} %psum.21), channel_id=1, replica_groups=mesh['grp'=2,'mode_0'=4,'mode_1'=16,'node'=2] {'mode_1'}, use_global_device_ids=true, to_apply=%region_4.0 | all-reduce | flops 2048 | bytes 16384 | tf_op jit(solution)/shard_map/psum | solution.py:16
  448.0 12.3 %psum.23 = f32[2048]{0:T(1024)S(1)} all-reduce(f32[2048]{0:T(1024)S(1)} %psum.22), channel_id=1, replica_groups=mesh['grp'=2,'mode_0'=4,'mode_1'=16,'node'=2] {'node'}, use_global_device_ids=true, to_apply=%region_5.0 | all-reduce | flops 2048 | bytes 16384 | tf_op jit(solution)/shard_map/psum | solution.py:16
  460.3 0.6 broadcast_multiply_fusion.2
  (17 shorter events, 0.1 us)
Async XLA Ops:
  5.8 212.3 %copy-start = (s32[2048]{0:T(1024)S(1)}, s32[2048]{0:T(1024)}, u32[]{:S(2)}) copy-start(s32[2048]{0:T(1024)} %param.9) | copy-start | bytes 24580
  5.8 212.3 %all-to-all-start = ((f32[64,64,256]{2,0,1:T(8,128)}), f32[64,64,256]{2,0,1:T(8,128)}, u32[]{:S(2)}, u32[]{:S(2)}) async-start(f32[64,64,256]{2,0,1:T(8,128)} %bitcast.7), calls=%async_computation | async-start | bytes 8388608 | tf_op jit(solution)/shard_map/all_to_all | solution.py:65
  218.0 194.2 %copy-start.1 = (f32[256]{0:T(256)S(1)}, f32[256]{0:T(256)}, u32[]{:S(2)}) copy-start(f32[256]{0:T(256)} %param.8) | copy-start | bytes 3076
where the time goes:
time: 462 us; the launch traced here: 461 us
  matrix products  194 us (42%)
  waiting for transfers between devices  182 us (39%)
  blocking collectives  46.4 us (10%)
  starting transfers between devices  29.7 us (6%)
  other arithmetic  4.88 us (1%)
    dot_general x8, matrix products, add_block(): lax.dot_general(rows, coeffs, (((0,), (0,)), ((), ())), precision=lax.Pre...  194 us
    all_to_all x1, waiting for transfers between devices, on_device(): lax.all_to_all(scaled, MODE, split_axis=1, concat_axis=0, tiled=True)  182 us
    psum x3, blocking collectives, over_axes(): return functools.reduce(lax.psum, axes, array)  46.4 us
    all_to_all x1, starting transfers between devices, on_device(): lax.all_to_all(scaled, MODE, split_axis=1, concat_axis=0, tiled=True)  29.7 us
  transfers between devices with their start and end apart: 1, of which 1 were waited for; matrix products, arithmetic and copies ran while one was open for 0% of the time, Pallas kernels for 0%

commit v1 on v0

v1 whole, which is shorter than its diff:
```python
import functools
import math

import jax
import jax.numpy as jnp
from jax import lax
from jax.experimental import pallas as pl
from jax.experimental.pallas import tpu as pltpu
from jax.sharding import PartitionSpec as P

MESH = pl.DeviceIdType.MESH
X, Z = 4, 16
C1, C2 = -1640531527, 668265261
H1, H2 = -2048144789, -1028477387
CHUNK = 256
GEN_ROWS, GEN_COLS = 16, 512


def wrap32(value):
    return ((value + 2**31) % 2**32) - 2**31


SINE_TURNS = (6.283185160089197, -41.3416550313564, 81.60100406980851, -76.54978221989163, 39.536705541154184)
SINE = [c * math.sqrt(2.0) for c in SINE_TURNS]


def mix(word):
    word = word ^ lax.shift_right_logical(word, 15)
    word = word * H1
    word = word ^ lax.shift_right_logical(word, 13)
    word = word * H2
    return word ^ lax.shift_right_logical(word, 16)


def normals_tile(seed_part, mode_part):
    start = seed_part + mode_part
    first = mix(start)
    second = mix(start + C2)
    unit = ((first & 16777215).astype(jnp.float32) + 0.5) * (1.0 / 16777216.0)
    minus_log = jnp.maximum(-jnp.log(unit), 1e-30)
    radius = minus_log * lax.rsqrt(minus_log)
    turn = (lax.shift_left(second, 8) | 128).astype(jnp.float32)
    w = 0.25 - jnp.abs(turn * (1.0 / 4294967296.0))
    s = w * w
    p = SINE[4]
    for c in (SINE[3], SINE[2], SINE[1], SINE[0]):
        p = p * s + c
    return radius * (p * w)


def kernel(
    groups, basis, scales, mean_log, seeds, out_hbm, means_out,
    send_buf, recv, chi, clo, acc, seed_rows, mode_col, part, bufa, s1, bufb, s2, bufc, fin,
    load_sem, tx_sem, rx_sem, ytx_sem, yrx_sem, red_tx, red_rx, out_sem,
):
    own = X * Z // groups
    per_chunk = CHUNK // 64
    own_chunks = own // per_chunk
    right_hops, left_hops = groups // 2, (groups - 1) // 2
    samples = seeds.shape[1]
    half = samples // 2

    grp = lax.axis_index("grp")
    me = lax.axis_index("mode")
    core = lax.axis_index("node")
    x, z = me // Z, lax.rem(me, Z)

    def displacement(plane, i):
        e = i * groups + plane
        zi = e // X
        k = (zi + 1) // 2
        dz = jnp.where(lax.rem(zi, 2) == 1, k, Z - k)
        return e, lax.rem(e, X), lax.rem(dz, Z)

    def peer(dx, dz, sign):
        px = lax.rem(x + sign * dx + X, X)
        pz = lax.rem(z + sign * dz + Z, Z)
        return px * Z + pz

    right = lax.rem(grp + 1, groups)
    left = lax.rem(grp + groups - 1, groups)

    def load(i):
        _, dx, dz = displacement(grp, i)
        col = pl.multiple_of(peer(dx, dz, 1) * 256, 256)
        return pltpu.make_async_copy(basis.at[:, pl.ds(col, 256)], send_buf.at[i], load_sem.at[i])

    @pl.loop(0, own)
    def _(i):
        load(i).start()

    bar = pltpu.get_barrier_semaphore()

    def hello(**where):
        pl.semaphore_signal(bar, 1, device_id=where, device_id_type=MESH)

    @pl.loop(0, own)
    def _(i):
        e, dx, dz = displacement(grp, i)

        @pl.when(e != 0)
        def _():
            hello(mode=peer(dx, dz, -1))

    @pl.loop(1, Z)
    def _(k):
        hello(mode=peer(0, k, 1))

    @pl.loop(1, X)
    def _(k):
        hello(mode=peer(k, 0, 1))

    hello(node=1 - core)
    if right_hops:
        hello(grp=left)
    if left_hops:
        hello(grp=right)

    row64 = lax.broadcasted_iota(jnp.int32, (64, 64), 0)
    col64 = lax.broadcasted_iota(jnp.int32, (64, 64), 1)
    scale_col = jnp.sum(
        jnp.where(row64 == col64, jnp.broadcast_to(scales[...], (64, 64)), 0.0), axis=1, keepdims=True
    )
    mode_col[...] = jnp.broadcast_to(scale_col, mode_col.shape)

    @pl.loop(0, own)
    def _(i):
        load(i).wait()
        send_buf[i] = send_buf[i] * mode_col[...]

    expected = jnp.where(grp == 0, own - 1, own) + (Z - 1) + (X - 1) + 1
    expected = expected + (1 if right_hops else 0) + (1 if left_hops else 0)
    pl.semaphore_wait(bar, expected)

    def piece(i):
        _, dx, dz = displacement(grp, i)
        return pltpu.make_async_remote_copy(
            src_ref=send_buf.at[i],
            dst_ref=recv.at[pl.ds(pl.multiple_of(i * 64, 64), 64), :],
            send_sem=tx_sem.at[i],
            recv_sem=rx_sem.at[i],
            device_id={"mode": peer(dx, dz, 1)},
            device_id_type=MESH,
        )

    @pl.loop(0, own)
    def _(i):
        e, _, _ = displacement(grp, i)

        @pl.when(e != 0)
        def _():
            piece(i).start()

        @pl.when(e == 0)
        def _():
            recv[0:64, :] = send_buf[0]

    def hop(source_block, target_block, i, to):
        src = pl.multiple_of((source_block * own + i) * 64, 64)
        dst = pl.multiple_of((target_block * own + i) * 64, 64)
        slot = (target_block - 1) * own + i
        return pltpu.make_async_remote_copy(
            src_ref=recv.at[pl.ds(src, 64), :],
            dst_ref=recv.at[pl.ds(dst, 64), :],
            send_sem=ytx_sem.at[slot],
            recv_sem=yrx_sem.at[slot],
            device_id={"grp": to},
            device_id_type=MESH,
        )

    nodes = acc.shape[0]
    row_n = lax.broadcasted_iota(jnp.int32, (nodes, nodes), 0)
    col_n = lax.broadcasted_iota(jnp.int32, (nodes, nodes), 1)
    mean_col = jnp.sum(
        jnp.where(row_n == col_n, jnp.broadcast_to(mean_log[...], (nodes, nodes)), 0.0), axis=1, keepdims=True
    )
    acc[...] = jnp.broadcast_to(mean_col, acc.shape)
    seed_rows[...] = jnp.broadcast_to(seeds[...] * C1, seed_rows.shape)

    row_ids = lax.broadcasted_iota(jnp.int32, (GEN_ROWS, GEN_COLS), 0) * wrap32(2 * C2)

    def generate(block, plane, chunk):
        @pl.loop(0, CHUNK // GEN_ROWS)
        def _(r):
            i = chunk * per_chunk + r // (64 // GEN_ROWS)
            _, dx, dz = displacement(plane, i)
            first_mode = peer(dx, dz, -1) * 64 + lax.rem(r, 64 // GEN_ROWS) * GEN_ROWS
            mode_part = row_ids + first_mode * wrap32(2 * C2)
            rows = pl.ds(pl.multiple_of(block * own * 64 + chunk * CHUNK + r * GEN_ROWS, GEN_ROWS), GEN_ROWS)
            for c in range(samples // GEN_COLS):
                cols = slice(c * GEN_COLS, (c + 1) * GEN_COLS)
                value = normals_tile(seed_rows[:, cols], mode_part)
                high = value.astype(jnp.bfloat16)
                chi[rows, cols] = high
                clo[rows, cols] = (value - high.astype(jnp.float32)).astype(jnp.bfloat16)

    def contract(block, chunk):
        rows = pl.ds(pl.multiple_of(block * own * 64 + chunk * CHUNK, CHUNK), CHUNK)
        lhs = recv[rows, :].T
        high = lhs.astype(jnp.bfloat16)
        low = (lhs - high.astype(jnp.float32)).astype(jnp.bfloat16)
        dot = functools.partial(jnp.dot, preferred_element_type=jnp.float32)
        for c in range(samples // 256):
            cols = slice(c * 256, (c + 1) * 256)
            c_high = chi[rows, cols]
            acc[:, cols] += dot(high, c_high) + dot(low, c_high) + dot(high, clo[rows, cols])

    def ring_block(b):
        hops = (b + 1) // 2
        to_right = lax.rem(b, 2) == 1
        plane = lax.rem(jnp.where(to_right, grp - hops, grp + hops) + groups, groups)
        return hops, to_right, plane

    def ring_forward(b, i):
        hops, to_right, _ = ring_block(b)

        @pl.when(jnp.logical_and(to_right, hops < right_hops))
        def _():
            hop(b, b + 2, i, right).start()

        @pl.when(jnp.logical_and(jnp.logical_not(to_right), hops < left_hops))
        def _():
            hop(b, b + 2, i, left).start()

    @pl.loop(0, own_chunks + 1)
    def _(j):
        @pl.when(j < own_chunks)
        def _():
            generate(0, grp, j)
            if groups > 1:
                generate(1, ring_block(1)[2], j)

            @pl.loop(0, per_chunk)
            def _(p):
                i = j * per_chunk + p
                e, _, _ = displacement(grp, i)

                @pl.when(e != 0)
                def _():
                    piece(i).wait()

                if right_hops:
                    hop(0, 1, i, right).start()
                if left_hops:
                    hop(0, 2, i, left).start()

            contract(0, j)

        if groups > 1:

            @pl.when(j > 0)
            def _():
                @pl.loop(1, groups)
                def _(b):
                    _, _, plane = ring_block(b)

                    @pl.when(b > 1)
                    def _():
                        generate(b, plane, j - 1)

                    @pl.loop(0, per_chunk)
                    def _(p):
                        i = (j - 1) * per_chunk + p
                        hop(b, b, i, right).wait()
                        ring_forward(b, i)

                    contract(b, j - 1)

    for c in range(samples // 256):
        cols = slice(c * 256, (c + 1) * 256)
        value = jnp.exp(acc[:, cols])
        acc[:, cols] = value
        part[:, cols] = jnp.sum(value, axis=0, keepdims=True)
    store = pltpu.make_async_copy(acc, out_hbm, out_sem)
    store.start()

    mine = pl.ds(pl.multiple_of(core * half, 128), half)
    other = pl.ds(pl.multiple_of((1 - core) * half, 128), half)
    swap = pltpu.make_async_remote_copy(
        src_ref=part.at[:, other], dst_ref=bufa, send_sem=red_tx.at[0], recv_sem=red_rx.at[0],
        device_id={"node": 1 - core}, device_id_type=MESH,
    )
    swap.start()
    swap.wait()
    s1[...] = part[:, mine] + bufa[...]

    def along(buffer, source, k, dx, dz, slot, row):
        return pltpu.make_async_remote_copy(
            src_ref=source, dst_ref=buffer.at[row], send_sem=red_tx.at[slot], recv_sem=red_rx.at[slot],
            device_id={"mode": peer(dx, dz, 1)}, device_id_type=MESH,
        )

    @pl.loop(1, X)
    def _(k):
        along(bufb, s1, k, k, 0, k, x).start()

    bufb[x] = s1[...]

    @pl.loop(1, X)
    def _(k):
        along(bufb, s1, k, k, 0, k, lax.rem(x + X - k, X)).wait()

    s2[...] = (bufb[0] + bufb[1]) + (bufb[2] + bufb[3])

    @pl.loop(1, Z)
    def _(k):
        along(bufc, s2, k, 0, k, X + k, z).start()

    bufc[z] = s2[...]

    @pl.loop(1, Z)
    def _(k):
        along(bufc, s2, k, 0, k, X + k, lax.rem(z + Z - k, Z)).wait()

    total = bufc[0]
    for k in range(1, Z):
        total = total + bufc[k]
    node_count = nodes * X * Z * 2
    fin[...] = total * (1.0 / node_count)
    back = pltpu.make_async_remote_copy(
        src_ref=fin, dst_ref=means_out.at[:, mine], send_sem=red_tx.at[X + Z], recv_sem=red_rx.at[X + Z],
        device_id={"node": 1 - core}, device_id_type=MESH,
    )
    back.start()
    means_out[:, mine] = fin[...]
    back.wait_send()
    pltpu.make_async_remote_copy(
        src_ref=fin, dst_ref=means_out.at[:, other], send_sem=red_tx.at[X + Z], recv_sem=red_rx.at[X + Z],
        device_id={"node": 1 - core}, device_id_type=MESH,
    ).wait_recv()
    store.wait()


def solution(mesh):
    groups = mesh.shape["grp"]

    def on_device(mode_basis, mode_scales, mean_log, sample_seeds):
        modes = mode_basis.shape[0]
        nodes, samples = mean_log.shape[0], sample_seeds.shape[0]
        all_modes = modes * X * Z
        own = X * Z // groups
        half = samples // 2
        f32 = jnp.float32
        vmem = pl.BlockSpec(memory_space=pltpu.VMEM)
        modulus, means = pl.pallas_call(
            functools.partial(kernel, groups),
            out_shape=(jax.ShapeDtypeStruct((nodes, samples), f32), jax.ShapeDtypeStruct((1, samples), f32)),
            in_specs=[pl.BlockSpec(memory_space=pl.ANY), vmem, vmem, vmem],
            out_specs=(pl.BlockSpec(memory_space=pl.ANY), vmem),
            scratch_shapes=[
                pltpu.VMEM((own, modes, nodes), f32),
                pltpu.VMEM((all_modes, nodes), f32),
                pltpu.VMEM((all_modes, samples), jnp.bfloat16),
                pltpu.VMEM((all_modes, samples), jnp.bfloat16),
                pltpu.VMEM((nodes, samples), f32),
                pltpu.VMEM((GEN_ROWS, samples), jnp.int32),
                pltpu.VMEM((modes, nodes), f32),
                pltpu.VMEM((1, samples), f32),
                pltpu.VMEM((1, half), f32),
                pltpu.VMEM((1, half), f32),
                pltpu.VMEM((X, 1, half), f32),
                pltpu.VMEM((1, half), f32),
                pltpu.VMEM((Z, 1, half), f32),
                pltpu.VMEM((1, half), f32),
                pltpu.SemaphoreType.DMA((own,)),
                pltpu.SemaphoreType.DMA((own,)),
                pltpu.SemaphoreType.DMA((own,)),
                pltpu.SemaphoreType.DMA((max(groups - 1, 1) * own,)),
                pltpu.SemaphoreType.DMA((max(groups - 1, 1) * own,)),
                pltpu.SemaphoreType.DMA((X + Z + 1,)),
                pltpu.SemaphoreType.DMA((X + Z + 1,)),
                pltpu.SemaphoreType.DMA,
            ],
            compiler_params=pltpu.CompilerParams(
                collective_id=0, has_side_effects=True, vmem_limit_bytes=60 * 1024 * 1024
            ),
        )(mode_basis, mode_scales[None, :], mean_log[None, :], sample_seeds[None, :])
        return modulus, means[0]

    return jax.shard_map(
        on_device,
        mesh=mesh,
        in_specs=(P("mode", "node"), P("mode"), P(("node", "mode")), P("grp")),
        out_specs=(P(("node", "mode"), "grp"), P("grp")),
        check_vma=False,
    )
```

time: 462 us -> 163 us (0.35)
  matrix products: 194 us -> 0 us
  waiting for transfers between devices: 182 us -> 0 us
  Pallas kernels: 0 us -> 158 us
  blocking collectives: 46.4 us -> 0 us
  starting transfers between devices: 29.7 us -> 0 us
  other arithmetic: 4.88 us -> 0 us
    dot_general x8 -> x0, matrix products: 194 us -> none  [add_block(): lax.dot_general(rows, coeffs, (((0,), (0,)), ((), ())), precision=lax.Pre...]
    all_to_all x1 -> x0, waiting for transfers between devices: 182 us -> none  [on_device(): lax.all_to_all(scaled, MODE, split_axis=1, concat_axis=0, tiled=True)]
    pallas_call x0 -> x1, Pallas kernels: none -> 158 us  [on_device(): pl.pallas_call(functools.partial(kernel, groups), out_shape=(jax.ShapeDty...]
    psum x3 -> x0, blocking collectives: 46.4 us -> none  [over_axes(): return functools.reduce(lax.psum, axes, array)]
    all_to_all x1 -> x0, starting transfers between devices: 29.7 us -> none  [on_device(): lax.all_to_all(scaled, MODE, split_axis=1, concat_axis=0, tiled=True)]
  transfers between devices with their start and end apart: 1 -> 0, of which waited for: 1 -> 0; matrix products, arithmetic and copies ran while one was open for 0% -> 0% of each run, Pallas kernels for 0% -> 0%
where the time goes in v1:
time: 163 us; the launch traced here: 162 us
  Pallas kernels  158 us (97%)
  local copies, waits for them, and re-layouts  3.74 us (2%)
    pallas_call x1, Pallas kernels, on_device(): pl.pallas_call(functools.partial(kernel, groups), out_shape=(jax.ShapeDty...  158 us
    unnamed x4, local copies, waits for them, and re-layouts  3.74 us

profile of v1, /device:TPU:33, one launch (start us, length us, event | category | flops | bytes accessed | tf_op | source)
XLA Modules:
  0.0 162.4 jit_solution(14504937143370196586)
XLA Ops:
  0.6 158.0 %shard_map.59 = (f32[256,2048]{1,0:T(8,128)}, f32[1,2048]{1,0:T(1,128)}) custom-call(f32[64,16384]{1,0:T(8,128)} %basis.1, f32[1,64]{1,0:T(1,128)} %bitcast.7, f32[1,256]{1,0:T(1,128)} %bitcast.6, s32[1,2048]{1,0:T(1,128)} %bitcast.4), custom_call_target="tpu_custom_call" | custom-call | tf_op jit(solution)/shard_map/pallas_call | solution.py:345
  158.7 0.0 copy-start
  158.7 3.1 %copy.8 = f32[256,2048]{1,0:T(8,128)} copy(f32[256,2048]{1,0:T(8,128)} %get-tuple-element.8) | data formatting | bytes 4194304
  161.8 0.0 copy-done
  161.8 0.6 copy.9
Async XLA Ops:
  158.7 3.2 %copy-start = (f32[1,2048]{1,0:T(1,128)S(1)}, f32[1,2048]{1,0:T(1,128)}, u32[]{:S(2)}) copy-start(f32[1,2048]{1,0:T(1,128)} %get-tuple-element.5) | copy-start | bytes 24580

commit v2 on v0

v2 whole, which is shorter than its diff:
```python
import functools
import math

import jax
import jax.numpy as jnp
from jax import lax
from jax.experimental import pallas as pl
from jax.experimental.pallas import tpu as pltpu
from jax.sharding import PartitionSpec as P

MESH = pl.DeviceIdType.MESH
X, Z = 4, 16
C1, C2 = -1640531527, 668265261
H1, H2 = -2048144789, -1028477387
OFFSETS = (8, 7, -7, 4, -4, 6, -6, 3, -3, 5, -5, 2, -2, 1, -1, 0)
SPLIT = 13
AHEAD = 3
LEAD = 9
GEN_ROWS, GEN_COLS = 16, 512


def pieces_sent(groups):
    if groups > X:
        return X * Z // groups
    return SPLIT * (X // groups) + (Z - SPLIT) * X


def wrap32(value):
    return ((value + 2**31) % 2**32) - 2**31


SINE_TURNS = (6.283185160089197, -41.3416550313564, 81.60100406980851, -76.54978221989163, 39.536705541154184)
SINE = [c * math.sqrt(2.0) for c in SINE_TURNS]


def mix(word):
    word = word ^ lax.shift_right_logical(word, 15)
    word = word * H1
    word = word ^ lax.shift_right_logical(word, 13)
    word = word * H2
    return word ^ lax.shift_right_logical(word, 16)


def normals_tile(seed_part, mode_part):
    start = seed_part + mode_part
    first = mix(start)
    second = mix(start + C2)
    unit = ((first & 16777215).astype(jnp.float32) + 0.5) * (1.0 / 16777216.0)
    minus_log = jnp.maximum(-jnp.log(unit), 1e-30)
    radius = minus_log * lax.rsqrt(minus_log)
    turn = (lax.shift_left(second, 8) | 128).astype(jnp.float32)
    w = 0.25 - jnp.abs(turn * (1.0 / 4294967296.0))
    s = w * w
    p = SINE[4]
    for c in (SINE[3], SINE[2], SINE[1], SINE[0]):
        p = p * s + c
    return radius * (p * w)


def kernel(
    groups, basis, scales, mean_log, seeds, out_hbm, means_out,
    small_s, small_m, small_d, send_buf, recv, chi, clo, acc, seed_rows, mode_col, part, row_buf, row_sum, col_buf, fin,
    in_sem, load_sem, tx_sem, rx_sem, ytx_sem, yrx_sem, red_tx, red_rx, out_sem,
):
    own = pieces_sent(groups)
    rows = basis.shape[0]
    chunk_rows = X * rows
    per = max(X // groups, 1)
    right_hops, left_hops = groups // 2, (groups - 1) // 2
    samples = seeds.shape[1]
    cores = lax.axis_size("node")
    nodes = acc.shape[0]

    grp = lax.axis_index("grp")
    me = lax.axis_index("mode")
    core = lax.axis_index("node")
    x, z = me // Z, lax.rem(me, Z)

    def wrap(value, size):
        return jnp.where(value >= size, value - size, value)

    def z_offset(t):
        if isinstance(t, int):
            return OFFSETS[t] % Z
        value = jnp.int32(OFFSETS[-1] % Z)
        for place, offset in enumerate(OFFSETS[:-1]):
            value = jnp.where(t == place, offset % Z, value)
        return value

    def number(plane, i):
        return i * groups + plane

    def ahead(dx, dz):
        return wrap(x + dx, X) * Z + wrap(z + dz, Z)

    def behind(dx, dz):
        return wrap(x - dx + X, X) * Z + wrap(z - dz + Z, Z)

    self_number = OFFSETS.index(0) * X

    def pieces_at(t):
        if t < SPLIT:
            return [(t * per + r, r * groups + grp) for r in range(per)]
        return [(SPLIT * per + (t - SPLIT) * X + dx, dx) for dx in range(X)]

    if groups <= X:
        pieces = [(i, t, dx) for t in range(len(OFFSETS)) for i, dx in pieces_at(t)]
        self_piece = SPLIT * per + (OFFSETS.index(0) - SPLIT) * X
    else:
        pieces = []
        for i in range(own):
            e = number(grp, i)
            pieces.append((i, lax.div(e, X), lax.rem(e, X)))
        self_piece = self_number // groups

    right = lax.rem(grp + 1, groups)
    left = lax.rem(grp + groups - 1, groups)

    bar = pltpu.get_barrier_semaphore()

    def hello(**where):
        pl.semaphore_signal(bar, 1, device_id=where, device_id_type=MESH)

    def row_peer(d):
        q = wrap(x * cores + core + d, X * cores)
        qx = lax.div(q, cores)
        return {"mode": qx * Z + z, "node": q - qx * cores}

    def load(i, t, dx):
        col = pl.multiple_of(ahead(dx, z_offset(t)) * nodes, nodes)
        return pltpu.make_async_copy(basis.at[:, pl.ds(col, nodes)], send_buf.at[i], load_sem.at[i])

    for args in pieces[: AHEAD + 1]:
        load(*args).start()

    columns = [r * groups + grp for r in range(per)] if groups <= X else range(X)

    @pl.loop(0, Z)
    def _(k):
        dz = wrap(k + Z // 2, Z)
        for dx in columns:

            @pl.when(jnp.logical_or(dz != 0, dx != 0))
            def _():
                hello(mode=behind(dx, dz))

        @pl.when(dz != 0)
        def _():
            hello(mode=behind(0, dz))

    beside = [(dx, dz) for dz in (1, Z - 1) for dx in range(1, X)] if groups <= X else []
    for dx, dz in beside:
        hello(mode=behind(dx, dz))

    small = [
        pltpu.make_async_copy(source, target, in_sem.at[k])
        for k, (source, target) in enumerate(((scales, small_s), (mean_log, small_m), (seeds, small_d)))
    ]
    for copy in small:
        copy.start()

    for args in pieces[AHEAD + 1 :]:
        load(*args).start()

    @pl.loop(1, X * cores)
    def _(d):
        hello(**row_peer(d))

    if right_hops:
        hello(grp=left)
    if left_hops:
        hello(grp=right)

    for copy in small:
        copy.wait()
    row64 = lax.broadcasted_iota(jnp.int32, (64, 64), 0)
    col64 = lax.broadcasted_iota(jnp.int32, (64, 64), 1)
    scale_col = jnp.sum(
        jnp.where(row64 == col64, jnp.broadcast_to(small_s[...], (64, 64)), 0.0), axis=1, keepdims=True
    )
    mode_col[...] = jnp.broadcast_to(scale_col, mode_col.shape)

    def scale(i):
        load(i, 0, 0).wait()
        send_buf[i] = send_buf[i] * mode_col[...]

    for i in range(min(AHEAD, own)):
        scale(i)

    own_columns = len(columns) if groups <= X else X
    no_self = jnp.where(grp == 0, 1, 0) if groups <= X else 1
    expected = Z * own_columns - no_self + (Z - 1) + len(beside) + (X * cores - 1)
    expected = expected + (1 if right_hops else 0) + (1 if left_hops else 0)
    pl.semaphore_wait(bar, expected)

    def slot(e):
        return recv.at[pl.ds(pl.multiple_of(e * rows, rows), rows), :]

    def piece(i, t, dx):
        return pltpu.make_async_remote_copy(
            src_ref=send_buf.at[i],
            dst_ref=slot(t * X + dx),
            send_sem=tx_sem.at[i],
            recv_sem=rx_sem.at[i],
            device_id={"mode": ahead(dx, z_offset(t))},
            device_id_type=MESH,
        )

    def send_piece(i, t, dx):
        @pl.when(t * X + dx != self_number)
        def _():
            piece(i, t, dx).start()

    for i, t, dx in pieces:
        if i + AHEAD < own:
            scale(i + AHEAD)
        send_piece(i, t, dx)

    has_self = True if groups <= X else grp == self_number % groups

    @pl.when(has_self)
    def _():
        recv[self_number * rows : (self_number + 1) * rows, :] = send_buf[self_piece]

    def hop(e, direction):
        return pltpu.make_async_remote_copy(
            src_ref=slot(e),
            dst_ref=slot(e),
            send_sem=ytx_sem.at[direction * X * Z + e],
            recv_sem=yrx_sem.at[e],
            device_id={"grp": (right, left)[direction]},
            device_id_type=MESH,
        )

    row_n = lax.broadcasted_iota(jnp.int32, (nodes, nodes), 0)
    col_n = lax.broadcasted_iota(jnp.int32, (nodes, nodes), 1)
    mean_col = jnp.sum(
        jnp.where(row_n == col_n, jnp.broadcast_to(small_m[...], (nodes, nodes)), 0.0), axis=1, keepdims=True
    )
    acc[...] = jnp.broadcast_to(mean_col, acc.shape)
    seed_rows[...] = jnp.broadcast_to(small_d[...] * C1, seed_rows.shape)

    row_ids = lax.broadcasted_iota(jnp.int32, (GEN_ROWS, GEN_COLS), 0) * wrap32(2 * C2)

    def generate(chunk):
        @pl.loop(0, X)
        def _(dx):
            first_mode = behind(dx, z_offset(chunk)) * rows
            first_row = (chunk * X + dx) * rows

            @pl.loop(0, rows // GEN_ROWS)
            def _(r):
                mode_part = row_ids + (first_mode + r * GEN_ROWS) * wrap32(2 * C2)
                at = pl.ds(pl.multiple_of(first_row + r * GEN_ROWS, GEN_ROWS), GEN_ROWS)
                for c in range(samples // GEN_COLS):
                    cols = slice(c * GEN_COLS, (c + 1) * GEN_COLS)
                    value = normals_tile(seed_rows[:, cols], mode_part)
                    high = value.astype(jnp.bfloat16)
                    chi[at, cols] = high
                    clo[at, cols] = (value - high.astype(jnp.float32)).astype(jnp.bfloat16)

    def contract(chunk):
        at = pl.ds(pl.multiple_of(chunk * chunk_rows, chunk_rows), chunk_rows)
        lhs = recv[at, :].T
        high = lhs.astype(jnp.bfloat16)
        low = (lhs - high.astype(jnp.float32)).astype(jnp.bfloat16)
        dot = functools.partial(jnp.dot, preferred_element_type=jnp.float32)
        for c in range(samples // 256):
            cols = slice(c * 256, (c + 1) * 256)
            c_high = chi[at, cols]
            acc[:, cols] += dot(high, c_high) + dot(low, c_high) + dot(high, clo[at, cols])

    def arrive(i, t, dx, travels=True):
        @pl.when(t * X + dx != self_number)
        def _():
            piece(i, t, dx).wait_recv()

        if travels and right_hops:
            hop(t * X + dx, 0).start()
        if travels and left_hops:
            hop(t * X + dx, 1).start()

    def ring_plane(b):
        hops = (b + 1) // 2
        return lax.rem(grp + (groups - hops if b % 2 else hops), groups)

    def goes_on(b):
        return (b + 1) // 2 < (right_hops if b % 2 else left_hops)

    chunks = len(OFFSETS)
    if groups <= X:

        @pl.loop(0, LEAD)
        def _(t):
            generate(t)

        @pl.loop(0, SPLIT + 1)
        def _(t):
            @pl.when(t < SPLIT)
            def _():
                for r in range(per):
                    arrive(t * per + r, t, r * groups + grp)

            @pl.when(t > 0)
            def _():
                for b in range(1, groups):
                    for r in range(per):
                        e = (t - 1) * X + r * groups + ring_plane(b)
                        hop(e, 0).wait_recv()
                        if goes_on(b):
                            hop(e, (b + 1) % 2).start()
                contract(t - 1)

            @pl.when(t + LEAD < chunks)
            def _():
                generate(t + LEAD)

        @pl.loop(SPLIT, chunks)
        def _(t):
            for dx in range(X):
                arrive(SPLIT * per + (t - SPLIT) * X + dx, t, dx, travels=False)
            contract(t)

    else:
        step = chunks // groups

        def generate_some(b):
            @pl.loop(0, step)
            def _(k):
                generate(b * step + k)

        generate_some(0)

        @pl.loop(0, own)
        def _(i):
            e = number(grp, i)
            t = lax.div(e, X)
            arrive(i, t, e - t * X)

        for b in range(1, groups):
            generate_some(b)

            @pl.loop(0, own)
            def _(i, b=b):
                e = number(ring_plane(b), i)
                hop(e, 0).wait_recv()
                if goes_on(b):
                    hop(e, (b + 1) % 2).start()

        @pl.loop(0, chunks)
        def _(t):
            contract(t)

    def all_sent():
        @pl.loop(0, own)
        def _(i):
            @pl.when(jnp.logical_not(jnp.logical_and(has_self, i == self_piece)))
            def _():
                piece(i, 0, 0).wait_send()

        @pl.loop(0, SPLIT * per if groups <= X else own)
        def _(i):
            e = number(grp, i)
            for direction, hops in enumerate((right_hops, left_hops)):
                if hops:
                    hop(e, direction).wait_send()
            for b in range(1, groups):
                if goes_on(b):
                    hop(number(ring_plane(b), i), (b + 1) % 2).wait_send()

    for c in range(samples // 256):
        cols = slice(c * 256, (c + 1) * 256)
        value = jnp.exp(acc[:, cols])
        acc[:, cols] = value
        part[c] = jnp.sum(value, axis=0, keepdims=True)
    store = pltpu.make_async_copy(acc, out_hbm, out_sem)
    store.start()

    me_row = x * cores + core
    width = X * cores

    def row_copy(source, target, d, slot):
        return pltpu.make_async_remote_copy(
            src_ref=source, dst_ref=target, send_sem=red_tx.at[slot], recv_sem=red_rx.at[slot],
            device_id=row_peer(d), device_id_type=MESH,
        )

    @pl.loop(1, width)
    def _(d):
        row_copy(part.at[wrap(me_row + d, width)], row_buf.at[me_row], d, d).start()

    row_buf[me_row] = part[me_row]

    @pl.loop(1, width)
    def _(d):
        row_copy(part.at[me_row], row_buf.at[me_row], d, d).wait()

    total = row_buf[0]
    for k in range(1, width):
        total = total + row_buf[k]
    row_sum[...] = total

    def column_copy(k):
        return pltpu.make_async_remote_copy(
            src_ref=row_sum, dst_ref=col_buf.at[z], send_sem=red_tx.at[width + k], recv_sem=red_rx.at[width + k],
            device_id={"mode": ahead(0, k)}, device_id_type=MESH,
        )

    for k in sorted(range(1, Z), key=lambda k: -min(k, Z - k)):
        column_copy(k).start()

    col_buf[z] = total

    @pl.loop(1, Z)
    def _(k):
        column_copy(k).wait()

    total = col_buf[0]
    for k in range(1, Z):
        total = total + col_buf[k]
    node_count = nodes * X * Z * cores
    fin[...] = total * (1.0 / node_count)

    @pl.loop(1, width)
    def _(d):
        row_copy(fin, means_out.at[me_row], d, width + Z + d).start()

    means_out[me_row] = fin[...]

    @pl.loop(1, width)
    def _(d):
        row_copy(fin, means_out.at[me_row], d, width + Z + d).wait()

    all_sent()
    store.wait()


def hand_over(modulus, means, modulus_out, means_out, held, held_means, in_sem, out_sem):
    parts = in_sem.shape[0] - 1
    rows = modulus.shape[0] // parts
    spans = [pl.ds(k * rows, rows) for k in range(parts)]
    steps = [(modulus.at[at], held.at[at], modulus_out.at[at]) for at in spans] + [(means, held_means, means_out)]
    copies_in = [pltpu.make_async_copy(a, b, in_sem.at[k]) for k, (a, b, _) in enumerate(steps)]
    copies_out = [pltpu.make_async_copy(b, c, out_sem.at[k]) for k, (_, b, c) in enumerate(steps)]
    for copy in copies_in:
        copy.start()
    for arrived, onward in zip(copies_in, copies_out):
        arrived.wait()
        onward.start()
    for copy in copies_out:
        copy.wait()


def solution(mesh):
    groups = mesh.shape["grp"]

    def on_device(mode_basis, mode_scales, mean_log, sample_seeds):
        modes = mode_basis.shape[0]
        nodes, samples = mean_log.shape[0], sample_seeds.shape[0]
        all_modes = modes * X * Z
        own = pieces_sent(groups)
        width = X * mesh.shape["node"]
        share = samples // width
        f32 = jnp.float32
        vmem = pl.BlockSpec(memory_space=pltpu.VMEM)
        modulus, means = pl.pallas_call(
            functools.partial(kernel, groups),
            out_shape=(jax.ShapeDtypeStruct((nodes, samples), f32), jax.ShapeDtypeStruct((width, 1, share), f32)),
            in_specs=[pl.BlockSpec(memory_space=pl.ANY)] * 4,
            out_specs=(pl.BlockSpec(memory_space=pl.ANY), vmem),
            scratch_shapes=[
                pltpu.VMEM((1, modes), f32),
                pltpu.VMEM((1, nodes), f32),
                pltpu.VMEM((1, samples), jnp.int32),
                pltpu.VMEM((own, modes, nodes), f32),
                pltpu.VMEM((all_modes, nodes), f32),
                pltpu.VMEM((all_modes, samples), jnp.bfloat16),
                pltpu.VMEM((all_modes, samples), jnp.bfloat16),
                pltpu.VMEM((nodes, samples), f32),
                pltpu.VMEM((GEN_ROWS, samples), jnp.int32),
                pltpu.VMEM((modes, nodes), f32),
                pltpu.VMEM((width, 1, share), f32),
                pltpu.VMEM((width, 1, share), f32),
                pltpu.VMEM((1, share), f32),
                pltpu.VMEM((Z, 1, share), f32),
                pltpu.VMEM((1, share), f32),
                pltpu.SemaphoreType.DMA((3,)),
                pltpu.SemaphoreType.DMA((own,)),
                pltpu.SemaphoreType.DMA((own,)),
                pltpu.SemaphoreType.DMA((own,)),
                pltpu.SemaphoreType.DMA((2 * X * Z,)),
                pltpu.SemaphoreType.DMA((X * Z,)),
                pltpu.SemaphoreType.DMA((2 * width + Z,)),
                pltpu.SemaphoreType.DMA((2 * width + Z,)),
                pltpu.SemaphoreType.DMA,
            ],
            compiler_params=pltpu.CompilerParams(
                collective_id=0, has_side_effects=True, vmem_limit_bytes=60 * 1024 * 1024
            ),
        )(mode_basis, mode_scales[None, :], mean_log[None, :], sample_seeds[None, :])
        parts = 4
        shapes = (jax.ShapeDtypeStruct(modulus.shape, f32), jax.ShapeDtypeStruct(means.shape, f32))
        modulus, means = pl.pallas_call(
            hand_over,
            out_shape=shapes,
            in_specs=[pl.BlockSpec(memory_space=pl.ANY)] * 2,
            out_specs=(pl.BlockSpec(memory_space=pl.ANY),) * 2,
            scratch_shapes=[
                pltpu.VMEM(modulus.shape, f32),
                pltpu.VMEM(means.shape, f32),
                pltpu.SemaphoreType.DMA((parts + 1,)),
                pltpu.SemaphoreType.DMA((parts + 1,)),
            ],
            compiler_params=pltpu.CompilerParams(vmem_limit_bytes=60 * 1024 * 1024),
        )(modulus, means)
        return modulus, means.reshape(samples)

    return jax.shard_map(
        on_device,
        mesh=mesh,
        in_specs=(P("mode", "node"), P("mode"), P(("node", "mode")), P("grp")),
        out_specs=(P(("node", "mode"), "grp"), P("grp")),
        check_vma=False,
    )
```

time: 462 us -> 155 us (0.34)
  matrix products: 194 us -> 0 us
  waiting for transfers between devices: 182 us -> 0 us
  Pallas kernels: 0 us -> 154 us
  blocking collectives: 46.4 us -> 0 us
  starting transfers between devices: 29.7 us -> 0 us
  other arithmetic: 4.88 us -> 0 us
    dot_general x8 -> x0, matrix products: 194 us -> none  [add_block(): lax.dot_general(rows, coeffs, (((0,), (0,)), ((), ())), precision=lax.Pre...]
    all_to_all x1 -> x0, waiting for transfers between devices: 182 us -> none  [on_device(): lax.all_to_all(scaled, MODE, split_axis=1, concat_axis=0, tiled=True)]
    pallas_call x0 -> x2, Pallas kernels: none -> 154 us  [the longest x1 151 us: on_device(): pl.pallas_call(functools.partial(kernel, groups), out_shape=(jax.ShapeDty...]
    psum x3 -> x0, blocking collectives: 46.4 us -> none  [over_axes(): return functools.reduce(lax.psum, axes, array)]
    all_to_all x1 -> x0, starting transfers between devices: 29.7 us -> none  [on_device(): lax.all_to_all(scaled, MODE, split_axis=1, concat_axis=0, tiled=True)]
  transfers between devices with their start and end apart: 1 -> 0, of which waited for: 1 -> 0; matrix products, arithmetic and copies ran while one was open for 0% -> 0% of each run, Pallas kernels for 0% -> 0%
where the time goes in v2:
time: 155 us; the launch traced here: 154 us
  Pallas kernels  154 us (99%)
    pallas_call x1, Pallas kernels, on_device(): pl.pallas_call(functools.partial(kernel, groups), out_shape=(jax.ShapeDty...  151 us

profile of v2, /device:TPU:33, one launch (start us, length us, event | category | flops | bytes accessed | tf_op | source)
XLA Modules:
  0.0 154.3 jit_solution(5469449480885413736)
XLA Ops:
  0.6 151.2 %shard_map.59 = (f32[256,2048]{1,0:T(8,128)}, f32[8,1,256]{2,1,0:T(1,128)}) custom-call(f32[64,16384]{1,0:T(8,128)} %basis.1, f32[1,64]{1,0:T(1,128)} %bitcast.6, f32[1,256]{1,0:T(1,128)} %bitcast.5, s32[1,2048]{1,0:T(1,128)} %bitcast.4), custom_call_target="tpu_custom_call" | custom-call | tf_op jit(solution)/shard_map/pallas_call | solution.py:466
  151.9 2.4 %shard_map.60 = (f32[256,2048]{1,0:T(8,128)}, f32[8,1,256]{2,1,0:T(1,128)}) custom-call(f32[256,2048]{1,0:T(8,128)} %get-tuple-element.6.modulus, f32[8,1,256]{2,1,0:T(1,128)} %get-tuple-element.7.means), custom_call_target="tpu_custom_call" | custom-call | tf_op jit(solution)/shard_map/pallas_call | solution.py:503

commit v3 on v2

--- a/solution.py
+++ b/solution.py
@@ -12,7 +12,9 @@
 X, Z = 4, 16
 C1, C2 = -1640531527, 668265261
 H1, H2 = -2048144789, -1028477387
-OFFSETS = (8, 7, -7, 4, -4, 6, -6, 3, -3, 5, -5, 2, -2, 1, -1, 0)
+OFFSETS = (4, -4, 3, -3, 8, 7, -7, 6, -6, 5, -5, 2, -2, 1, -1, 0)
+NEAR = 4
+NEAR_FIRST = 4
 SPLIT = 13
 AHEAD = 3
 LEAD = 9
@@ -60,7 +62,7 @@
 def kernel(
     groups, basis, scales, mean_log, seeds, out_hbm, means_out,
     small_s, small_m, small_d, send_buf, recv, chi, clo, acc, seed_rows, mode_col, part, row_buf, row_sum, col_buf, fin,
-    in_sem, load_sem, tx_sem, rx_sem, ytx_sem, yrx_sem, red_tx, red_rx, out_sem,
+    in_sem, load_sem, tx_sem, rx_sem, ytx_sem, yrx_sem, red_tx, red_rx, out_sem, far_sem,
 ):
     own = pieces_sent(groups)
     rows = basis.shape[0]
@@ -135,9 +137,9 @@
 
     columns = [r * groups + grp for r in range(per)] if groups <= X else range(X)
 
-    @pl.loop(0, Z)
+    @pl.loop(0, 2 * NEAR + 1)
     def _(k):
-        dz = wrap(k + Z // 2, Z)
+        dz = wrap(k + Z - NEAR, Z)
         for dx in columns:
 
             @pl.when(jnp.logical_or(dz != 0, dx != 0))
@@ -189,9 +191,12 @@
 
     own_columns = len(columns) if groups <= X else X
     no_self = jnp.where(grp == 0, 1, 0) if groups <= X else 1
-    expected = Z * own_columns - no_self + (Z - 1) + len(beside) + (X * cores - 1)
+    expected = (2 * NEAR + 1) * own_columns - no_self + 2 * NEAR + len(beside) + (X * cores - 1)
     expected = expected + (1 if right_hops else 0) + (1 if left_hops else 0)
     pl.semaphore_wait(bar, expected)
+
+    for side, dz in enumerate((Z - NEAR, NEAR)):
+        pl.semaphore_signal(far_sem.at[side], 1, device_id={"mode": ahead(0, dz)}, device_id_type=MESH)
 
     def slot(e):
         return recv.at[pl.ds(pl.multiple_of(e * rows, rows), rows), :]
@@ -211,7 +216,11 @@
         def _():
             piece(i, t, dx).start()
 
+    first_far = NEAR_FIRST * per if groups <= X else 0
     for i, t, dx in pieces:
+        if i == first_far:
+            for side in (0, 1):
+                pl.semaphore_wait(far_sem.at[side], 1)
         if i + AHEAD < own:
             scale(i + AHEAD)
         send_piece(i, t, dx)
@@ -493,6 +502,7 @@
                 pltpu.SemaphoreType.DMA((2 * width + Z,)),
                 pltpu.SemaphoreType.DMA((2 * width + Z,)),
                 pltpu.SemaphoreType.DMA,
+                pltpu.SemaphoreType.REGULAR((2,)),
             ],
             compiler_params=pltpu.CompilerParams(
                 collective_id=0, has_side_effects=True, vmem_limit_bytes=60 * 1024 * 1024

time: 155 us -> 152 us (0.981)
  Pallas kernels: 154 us -> 151 us
    pallas_call x1, Pallas kernels: 151 us -> 149 us  [on_device(): pl.pallas_call(functools.partial(kernel, groups), out_shape=(jax.ShapeDty...]
where the time goes in v3:
time: 152 us
  Pallas kernels  151 us (99%)
    pallas_call x1, Pallas kernels, on_device(): pl.pallas_call(functools.partial(kernel, groups), out_shape=(jax.ShapeDty...  149 us

profile of v3, /device:TPU:33, one launch (start us, length us, event | category | flops | bytes accessed | tf_op | source)
XLA Modules:
  0.0 151.6 jit_solution(7837643183380261256)
XLA Ops:
  0.6 148.5 %shard_map.59 = (f32[256,2048]{1,0:T(8,128)}, f32[8,1,256]{2,1,0:T(1,128)}) custom-call(f32[64,16384]{1,0:T(8,128)} %basis.1, f32[1,64]{1,0:T(1,128)} %bitcast.6, f32[1,256]{1,0:T(1,128)} %bitcast.5, s32[1,2048]{1,0:T(1,128)} %bitcast.4), custom_call_target="tpu_custom_call" | custom-call | tf_op jit(solution)/shard_map/pallas_call | solution.py:475
  149.1 2.4 %shard_map.60 = (f32[256,2048]{1,0:T(8,128)}, f32[8,1,256]{2,1,0:T(1,128)}) custom-call(f32[256,2048]{1,0:T(8,128)} %get-tuple-element.6.modulus, f32[8,1,256]{2,1,0:T(1,128)} %get-tuple-element.7.means), custom_call_target="tpu_custom_call" | custom-call | tf_op jit(solution)/shard_map/pallas_call | solution.py:513
